TPU v7x, 32 devices: a whole 2x2x4 slice. The times are simulated.
32 devices in a mesh: dp: 4 (over x, core), fsdp: 8 (over z, y).
Axes of the slice: x: 2, y: 2, z: 4, core: 2. Of those that a mesh axis runs over, the one named last changes fastest.
Arguments:
- tokens: bfloat16 [25088, 1024], P(('dp', 'fsdp')), may hold values from -6 to 6
- scale_codes: int32 [128], P(('dp', 'fsdp')), may hold values from 0 to 15
- w_qkv: float32 [1024, 3072], P('fsdp'), may hold values from -0.1875 to 0.1875
- b_q: float32 [1024], P('fsdp'), may hold values from -3 to 3
- b_v: float32 [1024], P('fsdp'), may hold values from -3 to 3
- w_out: float32 [1024, 1024], P('fsdp'), may hold values from -1.5 to 1.5
- b_out: float32 [1024], P('fsdp'), may hold values from -3 to 3
- gain_one: float32 [1024], P('fsdp'), may hold values from 0.5 to 1.5
- shift_one: float32 [1024], P('fsdp'), may hold values from -2 to 2
- w_fc1: float32 [1024, 4096], P('fsdp'), may hold values from -0.1875 to 0.1875
- b_fc1: float32 [4096], P('fsdp'), may hold values from -3 to 3
- w_fc2: float32 [4096, 1024], P('fsdp'), may hold values from -0.09375 to 0.09375
- b_fc2: float32 [1024], P('fsdp'), may hold values from -3 to 3
- gain_two: float32 [1024], P('fsdp'), may hold values from 0.5 to 1.5
- shift_two: float32 [1024], P('fsdp'), may hold values from -2 to 2
- cotangent: bfloat16 [25088, 1024], P(('dp', 'fsdp')), may hold values from -6 to 6
Outputs:
- block_out: bfloat16 [25088, 1024], P(('dp', 'fsdp'))
- grad_tokens: float32 [25088, 1024], P(('dp', 'fsdp'))
- grad_w_qkv: float32 [1024, 3072], P('fsdp')
- grad_b_q: float32 [1024], P('fsdp')
- grad_b_v: float32 [1024], P('fsdp')
- grad_w_out: float32 [1024, 1024], P('fsdp')
- grad_b_out: float32 [1024], P('fsdp')
- grad_gain_one: float32 [1024], P('fsdp')
- grad_shift_one: float32 [1024], P('fsdp')
- grad_w_fc1: float32 [1024, 4096], P('fsdp')
- grad_b_fc1: float32 [4096], P('fsdp')
- grad_w_fc2: float32 [4096, 1024], P('fsdp')
- grad_b_fc2: float32 [1024], P('fsdp')
- grad_gain_two: float32 [1024], P('fsdp')
- grad_shift_two: float32 [1024], P('fsdp')
All inputs are finite; a program needn't handle non-finite values.
Results may differ from a plain program's by a relative error of at most 0.015.
Values may be sent and summed in bfloat16 or wider, within the bound.
No kernel may reach another device: no remote copies, remote signals or barrier semaphores. Data moves between devices by JAX's collectives and lax.ppermute only.
A program may use at most 256 MiB of HBM per device.

v0:
```python
import math
import jax
import jax.numpy as jnp
from jax import lax
from jax.sharding import PartitionSpec as P

HEADS = 16
GRID = 14
NSCALE = 16
norm_eps = 1e-06


def positions(codes, grid_side, width):
    ratio = 0.3 * jnp.exp(codes.astype(jnp.float32) * (math.log(10.0 / 0.3) / (NSCALE - 1)))
    quarter = width // 4
    omega = jnp.exp(jnp.arange(quarter).astype(jnp.float32) * (-math.log(10000.0) / quarter))
    cells = jnp.arange(grid_side * grid_side, dtype=jnp.int32)
    row_place = (cells // grid_side).astype(jnp.float32)
    col_place = (cells % grid_side).astype(jnp.float32)
    row_angle = ratio[:, None, None] * row_place[None, :, None] * omega[None, None, :]
    col_angle = ratio[:, None, None] * col_place[None, :, None] * omega[None, None, :]
    return jnp.concatenate(
        [jnp.sin(row_angle), jnp.cos(row_angle), jnp.sin(col_angle), jnp.cos(col_angle)], axis=-1
    )


def norm_affine(hidden, gain, shift):
    center = jnp.mean(hidden, axis=-1, keepdims=True)
    offset = hidden - center
    spread = jnp.mean(offset * offset, axis=-1, keepdims=True)
    return offset * lax.rsqrt(spread + norm_eps) * gain + shift


def matmul(left, right):
    return jnp.dot(left, right, preferred_element_type=jnp.float32)


def inner_rows(left, right):
    return lax.dot_general(
        left, right, (((0,), (0,)), ((), ())), preferred_element_type=jnp.float32
    )


def times_transposed(left, right):
    return lax.dot_general(
        left, right, (((1,), (1,)), ((), ())), preferred_element_type=jnp.float32
    )


def column_total(values):
    return jnp.sum(values.astype(jnp.float32), axis=0)


def local(
    tokens,
    scale_codes,
    w_qkv,
    b_q,
    b_v,
    w_out,
    b_out,
    gain_one,
    shift_one,
    w_fc1,
    b_fc1,
    w_fc2,
    b_fc2,
    gain_two,
    shift_two,
    cotangent,
):
    half = jnp.bfloat16
    row_count, width = tokens.shape
    n_img = scale_codes.shape[0]
    patches = row_count // n_img
    head_size = width // HEADS
    factor = 1.0 / math.sqrt(head_size)
    place = positions(scale_codes, GRID, width).reshape(row_count, width)
    x_zero = tokens.astype(jnp.float32) + place
    attn_params = (
        lax.all_gather(w_qkv.astype(half), "fsdp", axis=0, tiled=True),
        lax.all_gather(b_q.astype(half), "fsdp", axis=0, tiled=True),
        lax.all_gather(b_v.astype(half), "fsdp", axis=0, tiled=True),
        lax.all_gather(w_out.astype(half), "fsdp", axis=0, tiled=True),
        lax.all_gather(b_out.astype(half), "fsdp", axis=0, tiled=True),
        lax.all_gather(gain_one.astype(half), "fsdp", axis=0, tiled=True),
        lax.all_gather(shift_one.astype(half), "fsdp", axis=0, tiled=True),
    )
    full_qkv, full_bq, full_bv, full_out, full_bout, full_gone, full_sone = attn_params
    gain_one_f = full_gone.astype(jnp.float32)
    shift_one_f = full_sone.astype(jnp.float32)
    normed_one = norm_affine(x_zero, gain_one_f, shift_one_f).astype(half)
    qkv_bias = jnp.concatenate([full_bq, jnp.zeros_like(full_bq), full_bv]).astype(jnp.float32)
    projected = (
        (matmul(normed_one, full_qkv) + qkv_bias)
        .astype(half)
        .reshape(n_img, patches, 3, HEADS, head_size)
    )
    queries = projected[:, :, 0]
    keys_all = projected[:, :, 1]
    values_all = projected[:, :, 2]
    scores = (
        jnp.einsum("iqhd,ikhd->ihqk", queries, keys_all, preferred_element_type=jnp.float32)
        * factor
    )
    top_score = jnp.max(scores, axis=-1, keepdims=True)
    raised = jnp.exp(scores - top_score)
    totals = jnp.sum(raised, axis=-1, keepdims=True)
    probs = raised / totals
    log_total = top_score + jnp.log(totals)
    mixed = jnp.einsum(
        "ihqk,ikhd->iqhd", probs.astype(half), values_all, preferred_element_type=jnp.float32
    )
    mixed = mixed.reshape(row_count, width).astype(half)
    after_attn = x_zero + (matmul(mixed, full_out) + full_bout.astype(jnp.float32))
    mlp_params = (
        lax.all_gather(w_fc1.astype(half), "fsdp", axis=0, tiled=True),
        lax.all_gather(b_fc1.astype(half), "fsdp", axis=0, tiled=True),
        lax.all_gather(w_fc2.astype(half), "fsdp", axis=0, tiled=True),
        lax.all_gather(b_fc2.astype(half), "fsdp", axis=0, tiled=True),
        lax.all_gather(gain_two.astype(half), "fsdp", axis=0, tiled=True),
        lax.all_gather(shift_two.astype(half), "fsdp", axis=0, tiled=True),
    )
    full_fc1, full_bfc1, full_fc2, full_bfc2, full_gtwo, full_stwo = mlp_params
    gain_two_f = full_gtwo.astype(jnp.float32)
    shift_two_f = full_stwo.astype(jnp.float32)
    normed_two = norm_affine(after_attn, gain_two_f, shift_two_f).astype(half)
    hidden_pre = matmul(normed_two, full_fc1) + full_bfc1.astype(jnp.float32)
    hidden_act = jax.nn.gelu(hidden_pre, approximate=False).astype(half)
    block_out = (
        after_attn + (matmul(hidden_act, full_fc2) + full_bfc2.astype(jnp.float32))
    ).astype(half)
    back_mlp = (
        lax.all_gather(w_fc1.astype(half), "fsdp", axis=0, tiled=True),
        lax.all_gather(b_fc1.astype(half), "fsdp", axis=0, tiled=True),
        lax.all_gather(w_fc2.astype(half), "fsdp", axis=0, tiled=True),
        lax.all_gather(b_fc2.astype(half), "fsdp", axis=0, tiled=True),
        lax.all_gather(gain_two.astype(half), "fsdp", axis=0, tiled=True),
        lax.all_gather(shift_two.astype(half), "fsdp", axis=0, tiled=True),
    )
    back_fc1 = back_mlp[0]
    back_fc2 = back_mlp[2]
    back_gtwo = back_mlp[4].astype(jnp.float32)
    back_stwo = back_mlp[5].astype(jnp.float32)
    grad_w_fc2 = inner_rows(hidden_act, cotangent)
    grad_b_fc2 = column_total(cotangent)
    grad_act = times_transposed(cotangent, back_fc2)
    unused_act, gelu_pull = jax.vjp(lambda pre: jax.nn.gelu(pre, approximate=False), hidden_pre)
    grad_pre = gelu_pull(grad_act)[0].astype(half)
    grad_w_fc1 = inner_rows(normed_two, grad_pre)
    grad_b_fc1 = column_total(grad_pre)
    grad_two_in = times_transposed(grad_pre, back_fc1)
    unused_two, norm_two_pull = jax.vjp(norm_affine, after_attn, back_gtwo, back_stwo)
    part_two, grad_gain_two, grad_shift_two = norm_two_pull(grad_two_in)
    grad_after = cotangent.astype(jnp.float32) + part_two
    mlp_shards = (
        lax.psum_scatter(grad_w_fc1, "fsdp", scatter_dimension=0, tiled=True),
        lax.psum_scatter(grad_b_fc1, "fsdp", scatter_dimension=0, tiled=True),
        lax.psum_scatter(grad_w_fc2, "fsdp", scatter_dimension=0, tiled=True),
        lax.psum_scatter(grad_b_fc2, "fsdp", scatter_dimension=0, tiled=True),
        lax.psum_scatter(grad_gain_two, "fsdp", scatter_dimension=0, tiled=True),
        lax.psum_scatter(grad_shift_two, "fsdp", scatter_dimension=0, tiled=True),
    )
    back_attn = (
        lax.all_gather(w_qkv.astype(half), "fsdp", axis=0, tiled=True),
        lax.all_gather(b_q.astype(half), "fsdp", axis=0, tiled=True),
        lax.all_gather(b_v.astype(half), "fsdp", axis=0, tiled=True),
        lax.all_gather(w_out.astype(half), "fsdp", axis=0, tiled=True),
        lax.all_gather(b_out.astype(half), "fsdp", axis=0, tiled=True),
        lax.all_gather(gain_one.astype(half), "fsdp", axis=0, tiled=True),
        lax.all_gather(shift_one.astype(half), "fsdp", axis=0, tiled=True),
    )
    back_qkv = back_attn[0]
    back_out = back_attn[3]
    back_gone = back_attn[5].astype(jnp.float32)
    back_sone = back_attn[6].astype(jnp.float32)
    branch_grad = grad_after.astype(half)
    grad_w_out = inner_rows(mixed, branch_grad)
    grad_b_out = column_total(branch_grad)
    grad_mixed = (
        times_transposed(branch_grad, back_out)
        .astype(half)
        .reshape(n_img, patches, HEADS, head_size)
    )
    again_scores = (
        jnp.einsum("iqhd,ikhd->ihqk", queries, keys_all, preferred_element_type=jnp.float32)
        * factor
    )
    again_probs = jnp.exp(again_scores - log_total)
    grad_values = jnp.einsum(
        "ihqk,iqhd->ikhd", again_probs.astype(half), grad_mixed, preferred_element_type=jnp.float32
    )
    grad_probs = jnp.einsum(
        "iqhd,ikhd->ihqk", grad_mixed, values_all, preferred_element_type=jnp.float32
    )
    weighted = jnp.sum(again_probs * grad_probs, axis=-1, keepdims=True)
    grad_scores = (again_probs * (grad_probs - weighted)).astype(half)
    grad_queries = (
        jnp.einsum("ihqk,ikhd->iqhd", grad_scores, keys_all, preferred_element_type=jnp.float32)
        * factor
    )
    grad_keys = (
        jnp.einsum("ihqk,iqhd->ikhd", grad_scores, queries, preferred_element_type=jnp.float32)
        * factor
    )
    grad_proj = (
        jnp.stack([grad_queries, grad_keys, grad_values], axis=2)
        .reshape(row_count, 3 * width)
        .astype(half)
    )
    grad_w_qkv = inner_rows(normed_one, grad_proj)
    grad_b_q = column_total(grad_proj[:, :width])
    grad_b_v = column_total(grad_proj[:, 2 * width :])
    grad_one_in = times_transposed(grad_proj, back_qkv)
    unused_one, norm_one_pull = jax.vjp(norm_affine, x_zero, back_gone, back_sone)
    part_one, grad_gain_one, grad_shift_one = norm_one_pull(grad_one_in)
    grad_tokens = grad_after + part_one
    attn_shards = (
        lax.psum_scatter(grad_w_qkv, "fsdp", scatter_dimension=0, tiled=True),
        lax.psum_scatter(grad_b_q, "fsdp", scatter_dimension=0, tiled=True),
        lax.psum_scatter(grad_b_v, "fsdp", scatter_dimension=0, tiled=True),
        lax.psum_scatter(grad_w_out, "fsdp", scatter_dimension=0, tiled=True),
        lax.psum_scatter(grad_b_out, "fsdp", scatter_dimension=0, tiled=True),
        lax.psum_scatter(grad_gain_one, "fsdp", scatter_dimension=0, tiled=True),
        lax.psum_scatter(grad_shift_one, "fsdp", scatter_dimension=0, tiled=True),
    )
    summed = (
        lax.psum(attn_shards[0].astype(jnp.bfloat16), "dp").astype(jnp.float32),
        lax.psum(attn_shards[1].astype(jnp.bfloat16), "dp").astype(jnp.float32),
        lax.psum(attn_shards[2].astype(jnp.bfloat16), "dp").astype(jnp.float32),
        lax.psum(attn_shards[3].astype(jnp.bfloat16), "dp").astype(jnp.float32),
        lax.psum(attn_shards[4].astype(jnp.bfloat16), "dp").astype(jnp.float32),
        lax.psum(attn_shards[5].astype(jnp.bfloat16), "dp").astype(jnp.float32),
        lax.psum(attn_shards[6].astype(jnp.bfloat16), "dp").astype(jnp.float32),
        lax.psum(mlp_shards[0].astype(jnp.bfloat16), "dp").astype(jnp.float32),
        lax.psum(mlp_shards[1].astype(jnp.bfloat16), "dp").astype(jnp.float32),
        lax.psum(mlp_shards[2].astype(jnp.bfloat16), "dp").astype(jnp.float32),
        lax.psum(mlp_shards[3].astype(jnp.bfloat16), "dp").astype(jnp.float32),
        lax.psum(mlp_shards[4].astype(jnp.bfloat16), "dp").astype(jnp.float32),
        lax.psum(mlp_shards[5].astype(jnp.bfloat16), "dp").astype(jnp.float32),
    )
    return (
        block_out,
        grad_tokens,
        summed[0],
        summed[1],
        summed[2],
        summed[3],
        summed[4],
        summed[5],
        summed[6],
        summed[7],
        summed[8],
        summed[9],
        summed[10],
        summed[11],
        summed[12],
    )


def solution(mesh):
    placed = (
        P(("dp", "fsdp"), None),
        P(("dp", "fsdp")),
        P("fsdp", None),
        P("fsdp"),
        P("fsdp"),
        P("fsdp", None),
        P("fsdp"),
        P("fsdp"),
        P("fsdp"),
        P("fsdp", None),
        P("fsdp"),
        P("fsdp", None),
        P("fsdp"),
        P("fsdp"),
        P("fsdp"),
        P(("dp", "fsdp"), None),
    )
    return jax.shard_map(
        local,
        mesh=mesh,
        in_specs=placed,
        out_specs=(
            P(("dp", "fsdp"), None),
            P(("dp", "fsdp"), None),
            P("fsdp", None),
            P("fsdp"),
            P("fsdp"),
            P("fsdp", None),
            P("fsdp"),
            P("fsdp"),
            P("fsdp"),
            P("fsdp", None),
            P("fsdp"),
            P("fsdp", None),
            P("fsdp"),
            P("fsdp"),
            P("fsdp"),
        ),
        check_vma=False,
    )
```

profile of v0, /device:TPU:0, one launch (start us, length us, event | category | flops | bytes accessed | tf_op | source)
XLA Modules:
  0.0 1432.2 jit_solution(16230341930971764661)
XLA Ops:
  7.2 2.5 convert_element_type.254
  13.0 2.7 convert_element_type.275
  16.1 22.5 %all-gather.6 = bf16[8,1,128]{2,1,0:T(2,128)(2,1)S(1)} all-gather(bf16[1,1,128]{2,1,0:T(2,128)(2,1)S(1)} %convert_bitcast_fusion.3), channel_id=1, replica_groups=mesh['dp'=4,'fsdp'=8] {'fsdp'}, dimensions={0}, use_global_device_ids=true | all-gather | bytes 2304 | tf_op jit(solution)/shard_map/all_gather | solution.py:122
  38.6 16.3 %all-gather.5 = bf16[8,1,128]{2,1,0:T(2,128)(2,1)S(1)} all-gather(bf16[1,1,128]{2,1,0:T(2,128)(2,1)S(1)} %convert_bitcast_fusion.4), channel_id=1, replica_groups=mesh['dp'=4,'fsdp'=8] {'fsdp'}, dimensions={0}, use_global_device_ids=true | all-gather | bytes 2304 | tf_op jit(solution)/shard_map/all_gather | solution.py:121
  54.9 18.5 %all-gather.1 = bf16[8,1,128]{2,1,0:T(2,128)(2,1)S(1)} all-gather(bf16[1,1,128]{2,1,0:T(2,128)(2,1)S(1)} %convert_bitcast_fusion.8), channel_id=1, replica_groups=mesh['dp'=4,'fsdp'=8] {'fsdp'}, dimensions={0}, use_global_device_ids=true | all-gather | bytes 2304 | tf_op jit(solution)/shard_map/all_gather | solution.py:87
  73.4 16.4 %all-gather = bf16[8,1,128]{2,1,0:T(2,128)(2,1)S(1)} all-gather(bf16[1,1,128]{2,1,0:T(2,128)(2,1)S(1)} %convert_bitcast_fusion.9), channel_id=1, replica_groups=mesh['dp'=4,'fsdp'=8] {'fsdp'}, dimensions={0}, use_global_device_ids=true | all-gather | bytes 2304 | tf_op jit(solution)/shard_map/all_gather | solution.py:86
  89.9 18.4 %all-gather.4 = bf16[8,1,128]{2,1,0:T(2,128)(2,1)S(1)} all-gather(bf16[1,1,128]{2,1,0:T(2,128)(2,1)S(1)} %convert_bitcast_fusion.5), channel_id=1, replica_groups=mesh['dp'=4,'fsdp'=8] {'fsdp'}, dimensions={0}, use_global_device_ids=true | all-gather | bytes 2304 | tf_op jit(solution)/shard_map/all_gather | solution.py:85
  108.3 16.2 %all-gather.3 = bf16[8,1,128]{2,1,0:T(2,128)(2,1)S(1)} all-gather(bf16[1,1,128]{2,1,0:T(2,128)(2,1)S(1)} %convert_bitcast_fusion.6), channel_id=1, replica_groups=mesh['dp'=4,'fsdp'=8] {'fsdp'}, dimensions={0}, use_global_device_ids=true | all-gather | bytes 2304 | tf_op jit(solution)/shard_map/all_gather | solution.py:83
  124.5 18.2 %all-gather.2 = bf16[8,1,128]{2,1,0:T(2,128)(2,1)S(1)} all-gather(bf16[1,1,128]{2,1,0:T(2,128)(2,1)S(1)} %convert_bitcast_fusion.7), channel_id=1, replica_groups=mesh['dp'=4,'fsdp'=8] {'fsdp'}, dimensions={0}, use_global_device_ids=true | all-gather | bytes 2304 | tf_op jit(solution)/shard_map/all_gather | solution.py:82
  142.8 26.3 %all-gather.7 = bf16[8,1,512]{2,1,0:T(2,128)(2,1)S(1)} all-gather(bf16[1,1,512]{2,1,0:T(2,128)(2,1)S(1)} %reshape.247), channel_id=1, replica_groups=mesh['dp'=4,'fsdp'=8] {'fsdp'}, dimensions={0}, use_global_device_ids=true | all-gather | bytes 9216 | tf_op jit(solution)/shard_map/all_gather | solution.py:118
  169.2 5.6 multiply_sine_fusion.1
  174.9 1.9 fusion.47
  177.3 10.6 add_convert_fusion.1
  187.9 12.7 reshape.267
  200.7 6.4 fusion.48
  207.1 3.7 copy.74
  210.8 4.3 copy.75
  215.1 5.9 copy.76
  221.0 3.6 multiply_reduce_fusion.1
  224.6 3.3 fusion.6
  230.4 3.4 convert_bitcast_fusion.1
  233.8 3.1 copy.58
  236.9 4.9 convert_element_type.262
  241.7 4.3 fusion.50
  248.2 41.3 %all-gather.18.cloned.1.call-done = bf16[1024,4096]{1,0:T(8,128)(2,1)} async-done(((bf16[128,4096]{1,0:T(8,128)(2,1)}), bf16[1024,4096]{1,0:T(8,128)(2,1)}) %all-gather.18.cloned.1.call-update) | async-done | bytes 8388624 | tf_op jit(solution)/shard_map/all_gather | solution.py:117
  289.5 13.2 fusion.42
  302.7 112.5 %all-gather.20.cloned.1.call-done = bf16[4096,1024]{1,0:T(8,128)(2,1)} async-done(((bf16[512,1024]{1,0:T(8,128)(2,1)}), bf16[4096,1024]{1,0:T(8,128)(2,1)}) %all-gather.20.cloned.1.call-update) | async-done | bytes 8388624 | tf_op jit(solution)/shard_map/all_gather | solution.py:119
  415.2 41.3 %convert_reduce_fusion = (f32[4096]{0:T(1024)}, bf16[784,4096]{1,0:T(8,128)(2,1)}, f32[784,4096]{1,0:T(8,128)}) fusion(f32[784,4096]{1,0:T(8,128)} %fusion.42, f32[4096]{0:T(1024)S(1)} %bitcast.97, bf16[784,1024]{1,0:T(8,128)(2,1)S(1)} %copy-done.12, bf16[4096,1024]{1,0:T(8,128)(2,1)} %all-gather.20.cloned.1.call-done), kind=kOutput, calls=%fused_computation.7 | convolution fusion | flops 6817509376 | bytes 42139648 | tf_op jit(solution)/shard_map/dot_general | solution.py:45
  456.5 10.6 multiply_reduce_fusion.2
  470.7 4.3 fusion.51
  476.0 3.4 convolution_convert_fusion
  479.4 3.4 reshape.268
  482.8 5.4 copy.60
  488.2 14.4 %multiply_reduce_fusion = (f32[4,16,196]{2,1,0:T(8,128)S(1)}, f32[4,16,196,196]{2,3,1,0:T(8,128)}) fusion(f32[4,16,196,196]{2,3,1,0:T(8,128)} %copy-done, f32[4,16,196]{2,1,0:T(8,128)S(1)} %log_add_fusion, bf16[4,196,16,64]{1,3,2,0:T(8,128)(2,1)} %copy.60, bf16[4,196,1,16,64]{1,4,3,0,2:T(8,128)(2,1)} %copy.74), kind=kOutput, calls=%fused_computation.2 | convolution fusion | flops 324525824 | bytes 22980608 | tf_op jit(solution)/shard_map/iqhd,ikhd->ihqk/dot_general | solution.py:193
  502.6 6.6 multiply_convert_fusion
  509.2 5.2 fusion.29
  514.4 4.3 fusion.26
  518.7 5.4 convert_bitcast_fusion
  524.1 4.4 pad_maximum_fusion
  528.5 9.1 copy.65
  537.6 12.7 convert_element_type.285
  550.4 13.0 fusion.40
  564.1 15.8 %fusion.41 = f32[1024,4096]{1,0:T(8,128)} fusion(bf16[784,4096]{1,0:T(8,128)(2,1)} %get-tuple-element.46, f32[784,1024]{1,0:T(8,128)} %copy-done.7, f32[1024]{0:T(1024)S(1)} %bitcast.110, f32[1024]{0:T(1024)S(1)} %bitcast.106, f32[784]{0:T(1024)S(1)} %fusion.33, f32[784]{0:T(1024)S(1)} %broadcast_multiply_fusion), kind=kOutput, calls=%fused_computation.116 | convolution fusion | flops 6580682752 | bytes 26425472 | tf_op jit(solution)/shard_map/dot_general | solution.py:39
  580.0 9.9 multiply_convert_fusion.1
  589.9 2.7 copy-done.11
  592.5 11.6 fusion.52
  606.7 18.6 %all-gather.8 = bf16[8,1,128]{2,1,0:T(2,128)(2,1)S(1)} all-gather(bf16[1,1,128]{2,1,0:T(2,128)(2,1)S(1)} %convert_bitcast_fusion.2), channel_id=1, replica_groups=mesh['dp'=4,'fsdp'=8] {'fsdp'}, dimensions={0}, use_global_device_ids=true | all-gather | bytes 2304 | tf_op jit(solution)/shard_map/all_gather | solution.py:120
  625.3 10.8 multiply_reduce_fusion.3
  637.2 2.8 convert_reduce_fusion.2
  640.3 2.4 convert_reduce_fusion.1
  642.7 36.8 %all-reduce.9 = (bf16[1024]{0:T(1024)(128)(2,1)S(1)}, bf16[1024]{0:T(1024)(128)(2,1)S(1)}, bf16[1024]{0:T(1024)(128)(2,1)S(1)}, bf16[1024]{0:T(1024)(128)(2,1)S(...) all-reduce(f32[1024]{0:T(1024)S(1)} %get-tuple-element.20, ...), channel_id=3, replica_groups=mesh['dp'=4,'fsdp'=8] {'fsdp'}, use_global_device_ids=true, to_apply=%region_14.15.clone | all-reduce | flops 12288 | bytes 73728
  680.2 6.3 all-reduce.10
  691.2 1.8 convert_element_type.294
  693.0 80.1 %reduce-scatter.5.cloned.1.call-done = f32[128,3072]{1,0:T(8,128)} async-done(((f32[1024,3072]{1,0:T(8,128)}), f32[128,3072]{1,0:T(8,128)}) %reduce-scatter.5.cloned.1.call-update) | async-done | bytes 1572880 | tf_op jit(solution)/shard_map/reduce_scatter | solution.py:219
  773.1 2.4 convert_element_type.286
  775.5 283.7 %reduce-scatter.9.cloned.1.call-done = f32[128,4096]{1,0:T(8,128)} async-done(((f32[1024,4096]{1,0:T(8,128)}), f32[128,4096]{1,0:T(8,128)}) %reduce-scatter.9.cloned.1.call-update) | async-done | bytes 2097168 | tf_op jit(solution)/shard_map/reduce_scatter | solution.py:157
  1059.2 2.7 convert_element_type.303
  1061.9 282.9 %reduce-scatter.11.cloned.1.call-done = f32[512,1024]{1,0:T(8,128)} async-done(((f32[4096,1024]{1,0:T(8,128)}), f32[512,1024]{1,0:T(8,128)}) %reduce-scatter.11.cloned.1.call-update) | async-done | bytes 2097168 | tf_op jit(solution)/shard_map/reduce_scatter | solution.py:159
  1344.8 2.7 convert_element_type.308
  1347.6 12.0 add_convert_fusion.2
  1359.5 57.2 %all-reduce.14.cloned.1.call-done = (bf16[128,3072]{1,0:T(8,128)(2,1)}, bf16[128,1024]{1,0:T(8,128)(2,1)}, bf16[128,4096]{1,0:T(8,128)(2,1)}, bf16[512,1024]{1,0:T(8,128)(2,1)}) async-done(((bf16[128,3072]{1,0:T(8,128)(2,1)}, bf16[128,1024]{1,0:T(8,128)(2,1)}, bf16[128,4096]{1,0:T(8,128)(2,1)}, bf16[512,1024]{1,0:T(8,128)(2,1)}), (bf16[128,3072]{1,0:T(8,128)(2,1)}, bf16[128,1024]{1,0:T(8,128)(2,1)}, ...) | async-done | bytes 3145744 | tf_op jit(solution)/shard_map/psum | solution.py:228
  1416.8 1.9 convert_element_type.295
  1418.7 2.4 convert_element_type.287
  1421.1 2.8 convert_element_type.304
  (195 shorter events, 23.7 us)
Async XLA Ops:
  7.2 4.6 copy-start.15
  7.2 170.1 %all-gather.14.cloned.1.call-start = ((), (), s32[]{:S(2)}) async-start(), calls=%async_computation.4 | async-start | bytes 7077888 | tf_op jit(solution)/shard_map/all_gather | solution.py:81
  9.8 232.0 %all-gather.16.cloned.1.call-start = ((), (), s32[]{:S(2)}) async-start(), calls=%async_computation.5 | async-start | bytes 2359296 | tf_op jit(solution)/shard_map/all_gather | solution.py:84
  11.6 4.1 copy-start.37
  11.7 4.4 copy-start.39
  11.7 26.9 %copy-start.40 = (f32[128]{0:T(128)S(1)}, f32[128]{0:T(128)}, u32[]{:S(2)}) copy-start(f32[128]{0:T(128)} %param.29) | copy-start | bytes 1540
  11.7 43.2 %copy-start.41 = (f32[128]{0:T(128)S(1)}, f32[128]{0:T(128)}, u32[]{:S(2)}) copy-start(f32[128]{0:T(128)} %param.24) | copy-start | bytes 1540
  11.7 61.7 %copy-start.42 = (f32[128]{0:T(128)S(1)}, f32[128]{0:T(128)}, u32[]{:S(2)}) copy-start(f32[128]{0:T(128)} %param.23) | copy-start | bytes 1540
  11.7 78.1 %copy-start.43 = (f32[128]{0:T(128)S(1)}, f32[128]{0:T(128)}, u32[]{:S(2)}) copy-start(f32[128]{0:T(128)} %param.22) | copy-start | bytes 1540
  11.7 96.5 %copy-start.44 = (f32[128]{0:T(128)S(1)}, f32[128]{0:T(128)}, u32[]{:S(2)}) copy-start(f32[128]{0:T(128)} %param.20) | copy-start | bytes 1540
  11.7 112.7 %copy-start.45 = (f32[128]{0:T(128)S(1)}, f32[128]{0:T(128)}, u32[]{:S(2)}) copy-start(f32[128]{0:T(128)} %param.19) | copy-start | bytes 1540
  11.7 130.9 %copy-start.46 = (s32[4]{0:T(128)S(1)}, s32[4]{0:T(128)}, u32[]{:S(2)}) copy-start(s32[4]{0:T(128)} %param.17) | copy-start | bytes 52
  11.7 277.7 %all-gather.18.cloned.1.call-start = ((), (), s32[]{:S(2)}) async-start(), calls=%async_computation.6 | async-start | bytes 9437184 | tf_op jit(solution)/shard_map/all_gather | solution.py:117
  12.9 402.3 %all-gather.20.cloned.1.call-start = ((), (), s32[]{:S(2)}) async-start(), calls=%async_computation.7 | async-start | bytes 9437184 | tf_op jit(solution)/shard_map/all_gather | solution.py:119
  15.7 675.5 %reduce-scatter.7.cloned.1.call-start = ((), (), s32[]{:S(2)}) async-start(), calls=%async_computation.9 | async-start | bytes 4718592 | tf_op jit(solution)/shard_map/reduce_scatter | solution.py:222
  38.5 250.9 %copy-start.33 = (f32[8,1,128]{2,1,0:T(1,128)}, f32[8,1,128]{2,1,0:T(1,128)S(1)}, u32[]{:S(2)}) copy-start(f32[8,1,128]{2,1,0:T(1,128)S(1)} %convert_element_type.320) | copy-start | bytes 12292
  73.4 103.9 %copy-start.35 = (f32[8,1,128]{2,1,0:T(1,128)}, f32[8,1,128]{2,1,0:T(1,128)S(1)}, u32[]{:S(2)}) copy-start(f32[8,1,128]{2,1,0:T(1,128)S(1)} %convert_element_type.317) | copy-start | bytes 12292
  89.8 87.5 %copy-start.28 = (f32[8,1,128]{2,1,0:T(1,128)}, f32[8,1,128]{2,1,0:T(1,128)S(1)}, u32[]{:S(2)}) copy-start(f32[8,1,128]{2,1,0:T(1,128)S(1)} %convert_element_type.316) | copy-start | bytes 12292
  176.7 11.2 copy-start.1
  176.8 11.1 copy-start.22
  177.2 10.7 copy-start.24
  177.3 10.6 copy-start.30
  215.1 9.5 copy-start.6
  224.6 5.1 copy-start
  224.6 5.1 copy-start.18
  224.6 5.7 copy-start.10
  229.7 0.6 copy-start.20
  233.7 8.0 copy-start.2
  246.0 1.7 copy-start.7
  248.2 54.5 %copy-start.26 = (f32[784]{0:T(1024)}, f32[784]{0:T(1024)S(1)}, u32[]{:S(2)}) copy-start(f32[784]{0:T(1024)S(1)} %multiply_reduce_fusion.6) | copy-start | bytes 9412
  289.5 125.7 %copy-start.12 = (bf16[784,1024]{1,0:T(8,128)(2,1)S(1)}, bf16[784,1024]{1,0:T(8,128)(2,1)}, u32[]{:S(2)}) copy-start(bf16[784,1024]{1,0:T(8,128)(2,1)} %param.31) | copy-start | bytes 4816900
  415.2 41.3 %copy-start.8 = (f32[784,1024]{1,0:T(8,128)S(1)}, f32[784,1024]{1,0:T(8,128)}, u32[]{:S(2)}) copy-start(f32[784,1024]{1,0:T(8,128)} %copy-done.7) | copy-start | bytes 9633796
  415.2 41.3 %copy-start.38 = (bf16[1024,4096]{1,0:T(8,128)(2,1)S(1)}, bf16[1024,4096]{1,0:T(8,128)(2,1)}, u32[]{:S(2)}) copy-start(bf16[1024,4096]{1,0:T(8,128)(2,1)} %all-gather.18.cloned.1.call-done) | copy-start | bytes 25165828
  456.5 10.6 copy-start.27
  468.1 1.7 copy-start.4
  468.1 2.7 copy-start.16
  475.1 0.8 copy-start.19
  475.1 0.9 copy-start.21
  475.1 298.0 %reduce-scatter.5.cloned.1.call-start = ((), (), s32[]{:S(2)}) async-start(), calls=%async_computation.8 | async-start | bytes 14155776 | tf_op jit(solution)/shard_map/reduce_scatter | solution.py:219
  482.8 19.8 %slice-start = ((s8[13107200]{0:T(1024)(128)(4,1)}), s8[524288]{0:T(1024)(128)(4,1)S(1)}, s32[]{:S(2)}) async-start(s8[13107200]{0:T(1024)(128)(4,1)} %bitcast.95), calls=%async_computation.13 | async-start | bytes 1048576
  488.2 14.4 %slice-start.1 = ((s8[13107200]{0:T(1024)(128)(4,1)}), s8[4194304]{0:T(1024)(128)(4,1)S(1)}, s32[]{:S(2)}) async-start(s8[13107200]{0:T(1024)(128)(4,1)} %bitcast.95), calls=%async_computation.14 | async-start | bytes 8388608
  488.2 14.4 %slice-start.2 = ((s8[13107200]{0:T(1024)(128)(4,1)}), s8[4194304]{0:T(1024)(128)(4,1)S(1)}, s32[]{:S(2)}) async-start(s8[13107200]{0:T(1024)(128)(4,1)} %bitcast.95), calls=%async_computation.15 | async-start | bytes 8388608
  488.2 14.4 %slice-start.3 = ((s8[13107200]{0:T(1024)(128)(4,1)}), s8[4194304]{0:T(1024)(128)(4,1)S(1)}, s32[]{:S(2)}) async-start(s8[13107200]{0:T(1024)(128)(4,1)} %bitcast.95), calls=%async_computation.16 | async-start | bytes 8388608
  537.6 12.7 copy-start.3
  537.6 12.7 copy-start.23
  537.6 12.7 copy-start.29
  537.6 12.7 copy-start.31
  537.6 12.7 copy-start.36
  563.4 0.7 copy-start.34
  563.4 495.8 %reduce-scatter.9.cloned.1.call-start = ((), (), s32[]{:S(2)}) async-start(), calls=%async_computation.10 | async-start | bytes 18874368 | tf_op jit(solution)/shard_map/reduce_scatter | solution.py:157
  579.9 764.9 %reduce-scatter.11.cloned.1.call-start = ((), (), s32[]{:S(2)}) async-start(), calls=%async_computation.11 | async-start | bytes 18874368 | tf_op jit(solution)/shard_map/reduce_scatter | solution.py:159
  579.9 12.6 copy-start.13
  589.9 2.7 copy-start.11
  604.1 0.7 copy-start.48
  604.1 2.5 copy-start.47
  604.1 812.6 %all-reduce.14.cloned.1.call-start = ((), (), s32[]{:S(2)}) async-start(), calls=%async_computation.12 | async-start | bytes 6291456 | tf_op jit(solution)/shard_map/psum | solution.py:228
  625.3 10.9 copy-start.25
  636.1 3.8 copy-start.14
  637.2 3.1 copy-start.5
  640.3 2.4 copy-start.32
  775.5 572.0 %copy-start.9 = (f32[784,1024]{1,0:T(8,128)S(1)}, f32[784,1024]{1,0:T(8,128)}, u32[]{:S(2)}) copy-start(f32[784,1024]{1,0:T(8,128)} %copy-done.7) | copy-start | bytes 9633796
  1416.8 7.1 copy-start.17
Sparse Core Ops, SparseCore 0:
  10.8 101.9 all-gather.13
  115.5 47.7 all-gather.15
  166.0 123.4 all-gather.17
  292.0 123.1 all-gather.19
  475.2 86.0 reduce-scatter.6
  565.2 207.8 reduce-scatter.4
  777.4 281.7 reduce-scatter.8
  1063.0 281.7 reduce-scatter.10
  1348.7 68.0 all-reduce.13
where the time goes:
time: 1440 us; the launch traced here: 1430 us
  waiting for transfers between devices  858 us (60%)
  blocking collectives  214 us (15%)
  matrix products  187 us (13%)
  local copies, waits for them, and re-layouts  84.6 us (6%)
  other arithmetic  71.7 us (5%)
  between operations  16.1 us (1%)
    reduce_scatter x1, waiting for transfers between devices, local(): lax.psum_scatter(grad_w_fc1, 'fsdp', scatter_dimension=0, tiled=True)  284 us
    reduce_scatter x1, waiting for transfers between devices, local(): lax.psum_scatter(grad_w_fc2, 'fsdp', scatter_dimension=0, tiled=True)  283 us
    all_gather x1, waiting for transfers between devices, local(): lax.all_gather(w_fc2.astype(half), 'fsdp', axis=0, tiled=True)  112 us
    reduce_scatter x1, waiting for transfers between devices, local(): lax.psum_scatter(grad_w_qkv, 'fsdp', scatter_dimension=0, tiled=True)  80.1 us
    dot_general x4, matrix products, times_transposed(): lax.dot_general(left, right, (((1,), (1,)), ((), ())), preferred_element_...  66.1 us
    psum x1, waiting for transfers between devices, local(): lax.psum(attn_shards[0].astype(jnp.bfloat16), 'dp').astype(jnp.float32)  57.2 us
    dot_general x4, matrix products, inner_rows(): lax.dot_general(left, right, (((0,), (0,)), ((), ())), preferred_element_...  44.7 us
    all_gather x1, waiting for transfers between devices, local(): lax.all_gather(w_fc1.astype(half), 'fsdp', axis=0, tiled=True)  41.3 us
  transfers between devices with their start and end apart: 9, of which 6 were waited for; matrix products, arithmetic and copies ran while one was open for 18% of the time, Pallas kernels for 0%

commit v1 on v0

--- a/solution.py
+++ b/solution.py
@@ -8,6 +8,19 @@
 GRID = 14
 NSCALE = 16
 norm_eps = 1e-06
+
+
+def ring_gather(value, axis, dim):
+    ways = lax.axis_size(axis)
+    up = [(d, (d + 1) % ways) for d in range(ways)]
+    down = [(d, (d - 1) % ways) for d in range(ways)]
+    earlier, later = ([value], [value])
+    for _ in range(ways // 2):
+        earlier.append(lax.ppermute(earlier[-1], axis, up))
+    for _ in range((ways - 1) // 2):
+        later.append(lax.ppermute(later[-1], axis, down))
+    line = jnp.concatenate([*earlier[::-1], *later[1:]], axis=dim)
+    return jnp.roll(line, (lax.axis_index(axis) - ways // 2) * value.shape[dim], axis=dim)
 
 
 def positions(codes, grid_side, width):
@@ -116,7 +129,7 @@
     mlp_params = (
         lax.all_gather(w_fc1.astype(half), "fsdp", axis=0, tiled=True),
         lax.all_gather(b_fc1.astype(half), "fsdp", axis=0, tiled=True),
-        lax.all_gather(w_fc2.astype(half), "fsdp", axis=0, tiled=True),
+        ring_gather(w_fc2.astype(half), "fsdp", 0),
         lax.all_gather(b_fc2.astype(half), "fsdp", axis=0, tiled=True),
         lax.all_gather(gain_two.astype(half), "fsdp", axis=0, tiled=True),
         lax.all_gather(shift_two.astype(half), "fsdp", axis=0, tiled=True),

time: 1440 us -> 1570 us (1.090)
  blocking collectives: 214 us -> 277 us
  starting transfers between devices: 0.37 us -> 36.5 us
  local copies, waits for them, and re-layouts: 84.6 us -> 114 us
    ppermute x0 -> x7, waiting for transfers between devices: none -> 162 us  [the longest x4 136 us: ring_gather(): earlier.append(lax.ppermute(earlier[-1], axis, up))]
    reduce_scatter x1, waiting for transfers between devices: 80.1 us -> 0.01 us  [local(): lax.psum_scatter(grad_w_qkv, 'fsdp', scatter_dimension=0, tiled=True)]
    reduce_scatter x1, waiting for transfers between devices: 284 us -> 215 us  [local(): lax.psum_scatter(grad_w_fc1, 'fsdp', scatter_dimension=0, tiled=True)]
    all_gather x1, blocking collectives: 18.6 us -> 58.3 us  [local(): lax.all_gather(b_fc2.astype(half), 'fsdp', axis=0, tiled=True)]
    ppermute x0 -> x7, starting transfers between devices: none -> 36.1 us  [the longest x3 30.5 us: ring_gather(): later.append(lax.ppermute(later[-1], axis, down))]
    unnamed x120 -> x155, local copies, waits for them, and re-layouts: 26.5 us -> 54.1 us
    unnamed x1, blocking collectives: 36.8 us -> 59.8 us
  transfers between devices with their start and end apart: 9 -> 16, of which waited for: 6 -> 9; matrix products, arithmetic and copies ran while one was open for 18% -> 18% of each run, Pallas kernels for 0% -> 0%
where the time goes in v1:
time: 1570 us
  waiting for transfers between devices  869 us (55%)
  blocking collectives  277 us (18%)
  matrix products  182 us (12%)
  local copies, waits for them, and re-layouts  114 us (7%)
  other arithmetic  71.1 us (5%)
  starting transfers between devices  36.5 us (2%)
  between operations  16.4 us (1%)
    reduce_scatter x1, waiting for transfers between devices, local(): lax.psum_scatter(grad_w_fc2, 'fsdp', scatter_dimension=0, tiled=True)  283 us
    reduce_scatter x1, waiting for transfers between devices, local(): lax.psum_scatter(grad_w_fc1, 'fsdp', scatter_dimension=0, tiled=True)  215 us
    ppermute x4, waiting for transfers between devices, ring_gather(): earlier.append(lax.ppermute(earlier[-1], axis, up))  136 us
    all_gather x1, waiting for transfers between devices, local(): lax.all_gather(w_fc2.astype(half), 'fsdp', axis=0, tiled=True)  112 us
    dot_general x4, matrix products, times_transposed(): lax.dot_general(left, right, (((1,), (1,)), ((), ())), preferred_element_...  61.9 us
    unnamed x1, blocking collectives  59.8 us
    all_gather x1, blocking collectives, local(): lax.all_gather(b_fc2.astype(half), 'fsdp', axis=0, tiled=True)  58.3 us
    psum x1, waiting for transfers between devices, local(): lax.psum(attn_shards[0].astype(jnp.bfloat16), 'dp').astype(jnp.float32)  57.2 us
  transfers between devices with their start and end apart: 16, of which 9 were waited for; matrix products, arithmetic and copies ran while one was open for 18% of the time, Pallas kernels for 0%

profile of v1, /device:TPU:0, one launch (start us, length us, event | category | flops | bytes accessed | tf_op | source)
XLA Modules:
  0.0 1565.5 jit_solution(7376552532512805987)
XLA Ops:
  11.8 2.7 convert_element_type.271
  16.2 22.5 %all-gather = bf16[8,1,128]{2,1,0:T(2,128)(2,1)S(1)} all-gather(bf16[1,1,128]{2,1,0:T(2,128)(2,1)S(1)} %convert_bitcast_fusion.9), channel_id=1, replica_groups=mesh['dp'=4,'fsdp'=8] {'fsdp'}, dimensions={0}, use_global_device_ids=true | all-gather | bytes 2304 | tf_op jit(solution)/shard_map/all_gather | solution.py:99
  38.7 16.3 %all-gather.1 = bf16[8,1,128]{2,1,0:T(2,128)(2,1)S(1)} all-gather(bf16[1,1,128]{2,1,0:T(2,128)(2,1)S(1)} %convert_bitcast_fusion.8), channel_id=1, replica_groups=mesh['dp'=4,'fsdp'=8] {'fsdp'}, dimensions={0}, use_global_device_ids=true | all-gather | bytes 2304 | tf_op jit(solution)/shard_map/all_gather | solution.py:100
  55.0 18.4 %all-gather.2 = bf16[8,1,128]{2,1,0:T(2,128)(2,1)S(1)} all-gather(bf16[1,1,128]{2,1,0:T(2,128)(2,1)S(1)} %convert_bitcast_fusion.7), channel_id=1, replica_groups=mesh['dp'=4,'fsdp'=8] {'fsdp'}, dimensions={0}, use_global_device_ids=true | all-gather | bytes 2304 | tf_op jit(solution)/shard_map/all_gather | solution.py:95
  73.5 16.4 %all-gather.3 = bf16[8,1,128]{2,1,0:T(2,128)(2,1)S(1)} all-gather(bf16[1,1,128]{2,1,0:T(2,128)(2,1)S(1)} %convert_bitcast_fusion.6), channel_id=1, replica_groups=mesh['dp'=4,'fsdp'=8] {'fsdp'}, dimensions={0}, use_global_device_ids=true | all-gather | bytes 2304 | tf_op jit(solution)/shard_map/all_gather | solution.py:96
  90.0 18.4 %all-gather.4 = bf16[8,1,128]{2,1,0:T(2,128)(2,1)S(1)} all-gather(bf16[1,1,128]{2,1,0:T(2,128)(2,1)S(1)} %convert_bitcast_fusion.5), channel_id=1, replica_groups=mesh['dp'=4,'fsdp'=8] {'fsdp'}, dimensions={0}, use_global_device_ids=true | all-gather | bytes 2304 | tf_op jit(solution)/shard_map/all_gather | solution.py:98
  108.4 16.2 %all-gather.5 = bf16[8,1,128]{2,1,0:T(2,128)(2,1)S(1)} all-gather(bf16[1,1,128]{2,1,0:T(2,128)(2,1)S(1)} %convert_bitcast_fusion.4), channel_id=1, replica_groups=mesh['dp'=4,'fsdp'=8] {'fsdp'}, dimensions={0}, use_global_device_ids=true | all-gather | bytes 2304 | tf_op jit(solution)/shard_map/all_gather | solution.py:134
  124.6 18.2 %all-gather.6 = bf16[8,1,128]{2,1,0:T(2,128)(2,1)S(1)} all-gather(bf16[1,1,128]{2,1,0:T(2,128)(2,1)S(1)} %convert_bitcast_fusion.3), channel_id=1, replica_groups=mesh['dp'=4,'fsdp'=8] {'fsdp'}, dimensions={0}, use_global_device_ids=true | all-gather | bytes 2304 | tf_op jit(solution)/shard_map/all_gather | solution.py:135
  142.8 26.3 %all-gather.7 = bf16[8,1,512]{2,1,0:T(2,128)(2,1)S(1)} all-gather(bf16[1,1,512]{2,1,0:T(2,128)(2,1)S(1)} %reshape.247), channel_id=1, replica_groups=mesh['dp'=4,'fsdp'=8] {'fsdp'}, dimensions={0}, use_global_device_ids=true | all-gather | bytes 9216 | tf_op jit(solution)/shard_map/all_gather | solution.py:131
  169.2 5.6 multiply_sine_fusion.1
  177.3 10.6 add_convert_fusion.1
  187.9 12.8 reshape.267
  200.7 6.9 fusion.53
  207.6 4.3 copy.75
  211.9 6.1 copy.76
  218.0 5.3 copy.74
  223.3 3.6 multiply_reduce_fusion.1
  226.9 3.3 fusion.6
  232.7 3.6 convert_bitcast_fusion.1
  236.3 3.1 copy.58
  239.4 4.9 convert_element_type.262
  244.3 4.3 fusion.55
  250.8 38.7 %all-gather.18.cloned.1.call-done = bf16[1024,4096]{1,0:T(8,128)(2,1)} async-done(((bf16[128,4096]{1,0:T(8,128)(2,1)}), bf16[1024,4096]{1,0:T(8,128)(2,1)}) %all-gather.18.cloned.1.call-update) | async-done | bytes 8388624 | tf_op jit(solution)/shard_map/all_gather | solution.py:130
  289.5 13.3 fusion.47
  302.8 112.4 %all-gather.20.cloned.1.call-done = bf16[4096,1024]{1,0:T(8,128)(2,1)} async-done(((bf16[512,1024]{1,0:T(8,128)(2,1)}), bf16[4096,1024]{1,0:T(8,128)(2,1)}) %all-gather.20.cloned.1.call-update) | async-done | bytes 8388624 | tf_op jit(solution)/shard_map/all_gather | solution.py:149
  415.2 41.1 %convert_reduce_fusion = (f32[4096]{0:T(1024)}, bf16[784,4096]{1,0:T(8,128)(2,1)}, f32[784,4096]{1,0:T(8,128)}) fusion(f32[784,4096]{1,0:T(8,128)} %fusion.47, f32[4096]{0:T(1024)S(1)} %bitcast.98, bf16[784,1024]{1,0:T(8,128)(2,1)S(1)} %copy-done.15, bf16[4096,1024]{1,0:T(8,128)(2,1)} %all-gather.20.cloned.1.call-done), kind=kOutput, calls=%fused_computation.7 | convolution fusion | flops 6817509376 | bytes 42139648 | tf_op jit(solution)/shard_map/dot_general | solution.py:58
  456.3 10.6 multiply_reduce_fusion.2
  470.2 4.3 fusion.56
  474.7 3.5 convolution_convert_fusion
  478.2 3.8 reshape.268
  481.9 5.3 copy.60
  487.3 14.4 multiply_reduce_fusion
  501.7 6.7 multiply_convert_fusion
  508.5 2.7 fusion.30
  511.2 5.2 fusion.33
  516.3 5.5 convert_bitcast_fusion
  521.8 4.4 pad_maximum_fusion
  526.2 8.9 copy.65
  535.1 12.7 convert_element_type.285
  547.8 13.1 fusion.45
  561.5 15.8 %fusion.46 = f32[1024,4096]{1,0:T(8,128)} fusion(bf16[784,4096]{1,0:T(8,128)(2,1)} %get-tuple-element.46, f32[784,1024]{1,0:T(8,128)} %copy-done.10, f32[1024]{0:T(1024)S(1)} %bitcast.114, f32[1024]{0:T(1024)S(1)} %bitcast.107, f32[784]{0:T(1024)S(1)} %fusion.37, f32[784]{0:T(1024)S(1)} %broadcast_multiply_fusion), kind=kOutput, calls=%fused_computation.135 | convolution fusion | flops 6580682752 | bytes 26425472 | tf_op jit(solution)/shard_map/dot_general | solution.py:52
  577.4 9.7 multiply_convert_fusion.1
  587.2 2.7 copy-done.14
  589.8 11.6 fusion.57
  602.0 50.6 %collective-permute-done = bf16[512,1024]{1,0:T(8,128)(2,1)S(1)} collective-permute-done((bf16[512,1024]{1,0:T(8,128)(2,1)}, bf16[512,1024]{1,0:T(8,128)(2,1)S(1)}, u32[]{:S(2)}, u32[]{:S(2)}) %collective-permute-start) | collective-permute-done | bytes 1048608 | tf_op jit(solution)/shard_map/ppermute | solution.py:19
  653.6 4.7 collective-permute-start.4
  658.3 48.4 %collective-permute-done.1 = bf16[512,1024]{1,0:T(8,128)(2,1)S(1)} collective-permute-done((bf16[512,1024]{1,0:T(8,128)(2,1)S(1)}, bf16[512,1024]{1,0:T(8,128)(2,1)S(1)}, u32[]{:S(2)}, u32[]{:S(2)}) %collective-permute-start.1) | collective-permute-done | bytes 1048608 | tf_op jit(solution)/shard_map/ppermute | solution.py:19
  710.2 22.3 %collective-permute-start.5 = (bf16[512,1024]{1,0:T(8,128)(2,1)}, bf16[512,1024]{1,0:T(8,128)(2,1)}, u32[]{:S(2)}, u32[]{:S(2)}) collective-permute-start(bf16[512,1024]{1,0:T(8,128)(2,1)} %collective-permute-done.4), channel_id=1, source_target_pairs={{0,7},{1,0},{2,1},{3,2},{4,3},{5,4},{6,5},{7,6},{8,15},{9,8},{10,9... | collective-permute-start | bytes 3145736 | tf_op jit(solution)/shard_map/ppermute | solution.py:21
  732.4 36.6 %collective-permute-done.2 = bf16[512,1024]{1,0:T(8,128)(2,1)} collective-permute-done((bf16[512,1024]{1,0:T(8,128)(2,1)S(1)}, bf16[512,1024]{1,0:T(8,128)(2,1)}, u32[]{:S(2)}, u32[]{:S(2)}) %collective-permute-start.2) | collective-permute-done | bytes 1048608 | tf_op jit(solution)/shard_map/ppermute | solution.py:19
  769.0 2.6 collective-permute-start.3
  773.5 58.3 %all-gather.8 = bf16[8,1,128]{2,1,0:T(2,128)(2,1)S(1)} all-gather(bf16[1,1,128]{2,1,0:T(2,128)(2,1)S(1)} %convert_bitcast_fusion.2), channel_id=1, replica_groups=mesh['dp'=4,'fsdp'=8] {'fsdp'}, dimensions={0}, use_global_device_ids=true | all-gather | bytes 2304 | tf_op jit(solution)/shard_map/all_gather | solution.py:133
  831.8 3.5 collective-permute-start.6
  849.0 26.8 %collective-permute-done.6 = bf16[512,1024]{1,0:T(8,128)(2,1)S(1)} collective-permute-done((bf16[512,1024]{1,0:T(8,128)(2,1)}, bf16[512,1024]{1,0:T(8,128)(2,1)S(1)}, u32[]{:S(2)}, u32[]{:S(2)}) %collective-permute-start.6) | collective-permute-done | bytes 1048608 | tf_op jit(solution)/shard_map/ppermute | solution.py:21
  890.6 6.8 multiply_reduce_fusion.3
  902.3 59.8 %all-reduce.9 = (bf16[1024]{0:T(1024)(128)(2,1)S(1)}, bf16[1024]{0:T(1024)(128)(2,1)S(1)}, bf16[1024]{0:T(1024)(128)(2,1)S(1)}, bf16[1024]{0:T(1024)(128)(2,1)S(...) all-reduce(f32[1024]{0:T(1024)S(1)} %get-tuple-element.20, ...), channel_id=3, replica_groups=mesh['dp'=4,'fsdp'=8] {'fsdp'}, use_global_device_ids=true, to_apply=%region_14.15.clone | all-reduce | flops 12288 | bytes 73728
  962.7 6.4 all-reduce.10
  978.1 215.0 %reduce-scatter.9.cloned.1.call-done = f32[128,4096]{1,0:T(8,128)} async-done(((f32[1024,4096]{1,0:T(8,128)}), f32[128,4096]{1,0:T(8,128)}) %reduce-scatter.9.cloned.1.call-update) | async-done | bytes 2097168 | tf_op jit(solution)/shard_map/reduce_scatter | solution.py:170
  1193.1 2.7 convert_element_type.303
  1195.8 283.0 %reduce-scatter.11.cloned.1.call-done = f32[512,1024]{1,0:T(8,128)} async-done(((f32[4096,1024]{1,0:T(8,128)}), f32[512,1024]{1,0:T(8,128)}) %reduce-scatter.11.cloned.1.call-update) | async-done | bytes 2097168 | tf_op jit(solution)/shard_map/reduce_scatter | solution.py:172
  1478.8 2.7 convert_element_type.308
  1481.5 12.0 add_convert_fusion.2
  1493.5 57.2 %all-reduce.14.cloned.1.call-done = (bf16[128,3072]{1,0:T(8,128)(2,1)}, bf16[128,1024]{1,0:T(8,128)(2,1)}, bf16[128,4096]{1,0:T(8,128)(2,1)}, bf16[512,1024]{1,0:T(8,128)(2,1)}) async-done(((bf16[128,3072]{1,0:T(8,128)(2,1)}, bf16[128,1024]{1,0:T(8,128)(2,1)}, bf16[128,4096]{1,0:T(8,128)(2,1)}, bf16[512,1024]{1,0:T(8,128)(2,1)}), (bf16[128,3072]{1,0:T(8,128)(2,1)}, bf16[128,1024]{1,0:T(8,128)(2,1)}, ...) | async-done | bytes 3145744 | tf_op jit(solution)/shard_map/psum | solution.py:241
  1550.8 2.8 convert_element_type.304
  1553.6 2.8 convert_element_type.309
  (249 shorter events, 68.3 us)
Async XLA Ops:
  7.2 7.4 copy-start.8
  7.2 8.8 copy-start.46
  7.2 9.0 copy-start.47
  7.2 31.4 %copy-start.48 = (f32[128]{0:T(128)S(1)}, f32[128]{0:T(128)}, u32[]{:S(2)}) copy-start(f32[128]{0:T(128)} %param.24) | copy-start | bytes 1540
  7.2 47.8 %copy-start.49 = (f32[128]{0:T(128)S(1)}, f32[128]{0:T(128)}, u32[]{:S(2)}) copy-start(f32[128]{0:T(128)} %param.19) | copy-start | bytes 1540
  7.2 66.3 %copy-start.50 = (f32[128]{0:T(128)S(1)}, f32[128]{0:T(128)}, u32[]{:S(2)}) copy-start(f32[128]{0:T(128)} %param.20) | copy-start | bytes 1540
  7.2 82.7 %copy-start.51 = (f32[128]{0:T(128)S(1)}, f32[128]{0:T(128)}, u32[]{:S(2)}) copy-start(f32[128]{0:T(128)} %param.22) | copy-start | bytes 1540
  7.3 101.1 %copy-start.52 = (f32[128]{0:T(128)S(1)}, f32[128]{0:T(128)}, u32[]{:S(2)}) copy-start(f32[128]{0:T(128)} %param.29) | copy-start | bytes 1540
  7.3 117.3 %copy-start.53 = (f32[128]{0:T(128)S(1)}, f32[128]{0:T(128)}, u32[]{:S(2)}) copy-start(f32[128]{0:T(128)} %param.30) | copy-start | bytes 1540
  7.3 135.5 %copy-start.44 = (f32[512]{0:T(512)S(1)}, f32[512]{0:T(512)}, u32[]{:S(2)}) copy-start(f32[512]{0:T(512)} %param.26) | copy-start | bytes 6148
  7.3 170.0 %all-gather.14.cloned.1.call-start = ((), (), s32[]{:S(2)}) async-start(), calls=%async_computation.4 | async-start | bytes 7077888 | tf_op jit(solution)/shard_map/all_gather | solution.py:94
  9.9 234.5 %all-gather.16.cloned.1.call-start = ((), (), s32[]{:S(2)}) async-start(), calls=%async_computation.5 | async-start | bytes 2359296 | tf_op jit(solution)/shard_map/all_gather | solution.py:97
  11.7 277.8 %all-gather.18.cloned.1.call-start = ((), (), s32[]{:S(2)}) async-start(), calls=%async_computation.6 | async-start | bytes 9437184 | tf_op jit(solution)/shard_map/all_gather | solution.py:130
  14.5 400.7 %all-gather.20.cloned.1.call-start = ((), (), s32[]{:S(2)}) async-start(), calls=%async_computation.7 | async-start | bytes 9437184 | tf_op jit(solution)/shard_map/all_gather | solution.py:149
  15.7 958.1 %reduce-scatter.7.cloned.1.call-start = ((), (), s32[]{:S(2)}) async-start(), calls=%async_computation.9 | async-start | bytes 4718592 | tf_op jit(solution)/shard_map/reduce_scatter | solution.py:235
  38.7 138.6 %copy-start.35 = (f32[8,1,128]{2,1,0:T(1,128)}, f32[8,1,128]{2,1,0:T(1,128)S(1)}, u32[]{:S(2)}) copy-start(f32[8,1,128]{2,1,0:T(1,128)S(1)} %convert_element_type.316) | copy-start | bytes 12292
  55.0 122.3 %copy-start.40 = (f32[8,1,128]{2,1,0:T(1,128)}, f32[8,1,128]{2,1,0:T(1,128)S(1)}, u32[]{:S(2)}) copy-start(f32[8,1,128]{2,1,0:T(1,128)S(1)} %convert_element_type.317) | copy-start | bytes 12292
  142.8 146.8 %copy-start.42 = (f32[8,1,128]{2,1,0:T(1,128)}, f32[8,1,128]{2,1,0:T(1,128)S(1)}, u32[]{:S(2)}) copy-start(f32[8,1,128]{2,1,0:T(1,128)S(1)} %convert_element_type.320) | copy-start | bytes 12292
  176.7 11.2 copy-start.1
  176.7 11.1 copy-start.29
  177.2 10.7 copy-start.31
  177.2 10.6 copy-start.37
  211.9 15.0 copy-start.6
  226.9 5.8 copy-start.13
  236.3 8.1 copy-start.2
  250.8 52.0 %copy-start.33 = (f32[784]{0:T(1024)}, f32[784]{0:T(1024)S(1)}, u32[]{:S(2)}) copy-start(f32[784]{0:T(1024)S(1)} %multiply_reduce_fusion.6) | copy-start | bytes 9412
  289.5 125.7 %copy-start.15 = (bf16[784,1024]{1,0:T(8,128)(2,1)S(1)}, bf16[784,1024]{1,0:T(8,128)(2,1)}, u32[]{:S(2)}) copy-start(bf16[784,1024]{1,0:T(8,128)(2,1)} %param.31) | copy-start | bytes 4816900
  415.2 41.1 %copy-start.11 = (f32[784,1024]{1,0:T(8,128)S(1)}, f32[784,1024]{1,0:T(8,128)}, u32[]{:S(2)}) copy-start(f32[784,1024]{1,0:T(8,128)} %copy-done.10) | copy-start | bytes 9633796
  415.2 41.1 %copy-start.45 = (bf16[1024,4096]{1,0:T(8,128)(2,1)S(1)}, bf16[1024,4096]{1,0:T(8,128)(2,1)}, u32[]{:S(2)}) copy-start(bf16[1024,4096]{1,0:T(8,128)(2,1)} %all-gather.18.cloned.1.call-done) | copy-start | bytes 25165828
  456.3 10.6 copy-start.34
  474.6 501.1 %reduce-scatter.5.cloned.1.call-start = ((), (), s32[]{:S(2)}) async-start(), calls=%async_computation.8 | async-start | bytes 14155776 | tf_op jit(solution)/shard_map/reduce_scatter | solution.py:232
  481.9 19.7 %slice-start = ((s8[13107200]{0:T(1024)(128)(4,1)}), s8[524288]{0:T(1024)(128)(4,1)S(1)}, s32[]{:S(2)}) async-start(s8[13107200]{0:T(1024)(128)(4,1)} %bitcast.94), calls=%async_computation.13 | async-start | bytes 1048576
  487.3 14.4 slice-start.1
  487.3 14.4 slice-start.2
  487.3 14.4 slice-start.3
  501.7 6.8 copy-start.7
  535.1 12.7 copy-start.3
  535.1 12.7 copy-start.30
  535.1 12.7 copy-start.36
  535.1 12.7 copy-start.38
  535.1 12.7 copy-start.41
  560.9 632.2 %reduce-scatter.9.cloned.1.call-start = ((), (), s32[]{:S(2)}) async-start(), calls=%async_computation.10 | async-start | bytes 18874368 | tf_op jit(solution)/shard_map/reduce_scatter | solution.py:170
  577.3 901.4 %reduce-scatter.11.cloned.1.call-start = ((), (), s32[]{:S(2)}) async-start(), calls=%async_computation.11 | async-start | bytes 18874368 | tf_op jit(solution)/shard_map/reduce_scatter | solution.py:172
  577.4 12.4 copy-start.16
  601.4 170.2 %copy-start.55 = (u32[32]{0:T(128)S(1)}, u32[32]{0:T(128)}, u32[]{:S(2)}) copy-start(u32[32]{0:T(128)} %constant.145) | copy-start | bytes 388
  601.4 172.1 %copy-start.54 = (f32[128]{0:T(128)S(1)}, f32[128]{0:T(128)}, u32[]{:S(2)}) copy-start(f32[128]{0:T(128)} %param.28) | copy-start | bytes 1540
  601.4 949.3 %all-reduce.14.cloned.1.call-start = ((), (), s32[]{:S(2)}) async-start(), calls=%async_computation.12 | async-start | bytes 6291456 | tf_op jit(solution)/shard_map/psum | solution.py:241
  601.5 51.2 %collective-permute-start = (bf16[512,1024]{1,0:T(8,128)(2,1)}, bf16[512,1024]{1,0:T(8,128)(2,1)S(1)}, u32[]{:S(2)}, u32[]{:S(2)}) collective-permute-start(bf16[512,1024]{1,0:T(8,128)(2,1)} %convert_element_type.275), channel_id=1, source_target_pairs={{0,1},{1,2},{2,3},{3,4},{4,5},{5,6},{6,7},{7,0},{8,9},{9,10},{10,1... | collective-permute-start | bytes 3145736 | tf_op jit(solution)/shard_map/ppermute | solution.py:19
  653.6 53.1 %collective-permute-start.1 = (bf16[512,1024]{1,0:T(8,128)(2,1)S(1)}, bf16[512,1024]{1,0:T(8,128)(2,1)S(1)}, u32[]{:S(2)}, u32[]{:S(2)}) collective-permute-start(bf16[512,1024]{1,0:T(8,128)(2,1)S(1)} %collective-permute-done), channel_id=1, source_target_pairs={{0,1},{1,2},{2,3},{3,4},{4,5},{5,6},{6,7},{7,0},{8,9},{9,10},{10,1... | collective-permute-start | bytes 3145736 | tf_op jit(solution)/shard_map/ppermute | solution.py:19
  653.6 56.5 %collective-permute-start.4 = (bf16[512,1024]{1,0:T(8,128)(2,1)}, bf16[512,1024]{1,0:T(8,128)(2,1)}, u32[]{:S(2)}, u32[]{:S(2)}) collective-permute-start(bf16[512,1024]{1,0:T(8,128)(2,1)} %convert_element_type.275), channel_id=1, source_target_pairs={{0,7},{1,0},{2,1},{3,2},{4,3},{5,4},{6,5},{7,6},{8,15},{9,8},{10,9... | collective-permute-start | bytes 3145736 | tf_op jit(solution)/shard_map/ppermute | solution.py:21
  707.7 61.4 %collective-permute-start.2 = (bf16[512,1024]{1,0:T(8,128)(2,1)S(1)}, bf16[512,1024]{1,0:T(8,128)(2,1)}, u32[]{:S(2)}, u32[]{:S(2)}) collective-permute-start(bf16[512,1024]{1,0:T(8,128)(2,1)S(1)} %collective-permute-done.1), channel_id=1, source_target_pairs={{0,1},{1,2},{2,3},{3,4},{4,5},{5,6},{6,7},{7,0},{8,9},{9,10},{10,1... | collective-permute-start | bytes 3145736 | tf_op jit(solution)/shard_map/ppermute | solution.py:19
  710.2 121.7 %collective-permute-start.5 = (bf16[512,1024]{1,0:T(8,128)(2,1)}, bf16[512,1024]{1,0:T(8,128)(2,1)}, u32[]{:S(2)}, u32[]{:S(2)}) collective-permute-start(bf16[512,1024]{1,0:T(8,128)(2,1)} %collective-permute-done.4), channel_id=1, source_target_pairs={{0,7},{1,0},{2,1},{3,2},{4,3},{5,4},{6,5},{7,6},{8,15},{9,8},{10,9... | collective-permute-start | bytes 3145736 | tf_op jit(solution)/shard_map/ppermute | solution.py:21
  769.0 66.3 %collective-permute-start.3 = (bf16[512,1024]{1,0:T(8,128)(2,1)}, bf16[512,1024]{1,0:T(8,128)(2,1)}, u32[]{:S(2)}, u32[]{:S(2)}) collective-permute-start(bf16[512,1024]{1,0:T(8,128)(2,1)} %collective-permute-done.2), channel_id=1, source_target_pairs={{0,1},{1,2},{2,3},{3,4},{4,5},{5,6},{6,7},{7,0},{8,9},{9,10},{10,1... | collective-permute-start | bytes 3145736 | tf_op jit(solution)/shard_map/ppermute | solution.py:19
  831.8 10.4 copy-start.19
  831.8 11.4 copy-start.9
  831.8 43.9 %collective-permute-start.6 = (bf16[512,1024]{1,0:T(8,128)(2,1)}, bf16[512,1024]{1,0:T(8,128)(2,1)S(1)}, u32[]{:S(2)}, u32[]{:S(2)}) collective-permute-start(bf16[512,1024]{1,0:T(8,128)(2,1)} %collective-permute-done.5), channel_id=1, source_target_pairs={{0,7},{1,0},{2,1},{3,2},{4,3},{5,4},{6,5},{7,6},{8,15},{9,8},{10,9... | collective-permute-start | bytes 3145736 | tf_op jit(solution)/shard_map/ppermute | solution.py:21
  843.3 38.3 %copy-start.21 = (bf16[512,1024]{1,0:T(8,128)(2,1)S(1)}, bf16[512,1024]{1,0:T(8,128)(2,1)}, u32[]{:S(2)}) copy-start(bf16[512,1024]{1,0:T(8,128)(2,1)} %copy-done.20) | copy-start | bytes 3145732
  876.8 13.8 slice-start.6
  881.5 9.1 slice-start.4
  883.6 7.0 slice-start.5
  883.6 7.0 slice-start.7
  890.6 6.8 copy-start.32
  973.8 507.7 %copy-start.12 = (f32[784,1024]{1,0:T(8,128)S(1)}, f32[784,1024]{1,0:T(8,128)}, u32[]{:S(2)}) copy-start(f32[784,1024]{1,0:T(8,128)} %copy-done.10) | copy-start | bytes 9633796
  1550.8 6.9 copy-start.28
  (16 other events, 45.0 us)
Sparse Core Ops, SparseCore 0:
  10.9 101.9 all-gather.13
  115.6 47.7 all-gather.15
  166.1 123.3 all-gather.17
  292.1 123.1 all-gather.19
  474.7 86.0 reduce-scatter.6
  564.7 340.5 reduce-scatter.4
  909.6 283.4 reduce-scatter.8
  1196.9 281.8 reduce-scatter.10
  1482.7 68.0 all-reduce.13
